TPU v7x, 32 devices: a whole 2x2x4 slice. The times are simulated.
32 devices in a mesh: seq: 8 (over z, core), fsdp: 4 (over y, x).
Axes of the slice: x: 2, y: 2, z: 4, core: 2. Of those that a mesh axis runs over, the one named last changes fastest.
Arguments:
- block_input: bfloat16 [8, 1472, 1152], P('fsdp', 'seq')
- key_mask: int32 [16, 736], P('fsdp'), may hold values from 0 to 1, as said below
- slot_flags: int32 [16], P('fsdp'), may hold values from 0 to 1, as said below
- norm1_gain: bfloat16 [1152], P('fsdp'), may hold values from 0.5 to 1.5
- norm1_bias: bfloat16 [1152], P('fsdp'), may hold values from -3 to 3
- qkv_weight: bfloat16 [1152, 3456], P('fsdp'), may hold values from -0.25 to 0.25
- query_bias: bfloat16 [1152], P('fsdp'), may hold values from -3 to 3
- value_bias: bfloat16 [1152], P('fsdp'), may hold values from -3 to 3
- proj_weight: bfloat16 [1152, 1152], P('fsdp'), may hold values from -0.375 to 0.375
- proj_bias: bfloat16 [1152], P('fsdp'), may hold values from -3 to 3
- norm2_gain: bfloat16 [1152], P('fsdp'), may hold values from 0.5 to 1.5
- norm2_bias: bfloat16 [1152], P('fsdp'), may hold values from -3 to 3
- up_weight: bfloat16 [1152, 4304], P('fsdp'), may hold values from -0.1875 to 0.1875
- up_bias: bfloat16 [4304], P('fsdp'), may hold values from -3 to 3
- down_weight: bfloat16 [4304, 1152], P(None, 'fsdp'), may hold values from -0.09375 to 0.09375
- down_bias: bfloat16 [1152], P('fsdp'), may hold values from -3 to 3
- out_grad: bfloat16 [8, 1472, 1152], P('fsdp', 'seq'), may hold values from -6 to 6
Outputs:
- block_output: bfloat16 [8, 1472, 1152], P('fsdp', 'seq')
- input_grad: float32 [8, 1472, 1152], P('fsdp', 'seq')
- norm1_gain_grad: float32 [1152], P('fsdp')
- norm1_bias_grad: float32 [1152], P('fsdp')
- qkv_weight_grad: float32 [1152, 3456], P('fsdp')
- query_bias_grad: float32 [1152], P('fsdp')
- value_bias_grad: float32 [1152], P('fsdp')
- proj_weight_grad: float32 [1152, 1152], P('fsdp')
- proj_bias_grad: float32 [1152], P('fsdp')
- norm2_gain_grad: float32 [1152], P('fsdp')
- norm2_bias_grad: float32 [1152], P('fsdp')
- up_weight_grad: float32 [1152, 4304], P('fsdp')
- up_bias_grad: float32 [4304], P('fsdp')
- down_weight_grad: float32 [4304, 1152], P(None, 'fsdp')
- down_bias_grad: float32 [1152], P('fsdp')
Inputs may be any that keep to these rules, and one draw needn't show every extreme that they name: `key_mask`: positions 729 and beyond are 0 in every slot; every position of a slot whose flag is 0 is 0. `slot_flags`: exactly max(1, 1) slots have flag 0, at places drawn from the seed.
All inputs are finite; a program needn't handle non-finite values.
Results may differ from a plain program's by a relative error of at most 0.012.
The roundings to bfloat16 on the way count: a program that leaves them out, or rounds other values in their place, can miss the bound.
Values may be sent and summed in bfloat16 or wider, within the bound.
A program may use at most 256 MiB of HBM per device.

v0:
```python
import jax
import jax.numpy as jnp
from jax import lax
from jax.sharding import Mesh
from jax.sharding import PartitionSpec as P

HEADS = 16
HEAD = 72
epsilon = 1e-06
SEQ = ("zh", "zl", "core")
ZAX = ("zh", "zl")
GROUP = ("zl", "core")


def layer_norm(values, gain_vec, bias_vec):
    row_mean = jnp.mean(values, axis=-1, keepdims=True)
    centered = values - row_mean
    variance = jnp.mean(centered * centered, axis=-1, keepdims=True)
    return centered * lax.rsqrt(variance + epsilon) * gain_vec + bias_vec


def gelu_tanh(values):
    return (
        0.5
        * values
        * (1.0 + jnp.tanh(0.7978845608028654 * (values + 0.044715 * values * values * values)))
    )


def core_swap(x):
    return lax.ppermute(x, "core", [(0, 1), (1, 0)])


def in_core_order(mine, other):
    first = lax.axis_index("core") == 0
    return (jnp.where(first, mine, other), jnp.where(first, other, mine))


def gather_weight(w):
    rows, cols = w.shape
    half = rows // 2
    piece = lax.dynamic_slice_in_dim(w, lax.axis_index("core") * half, half, axis=0)
    mine = lax.all_gather(piece, "fsdp", axis=0, tiled=False)
    other = core_swap(mine)
    first, second = in_core_order(mine, other)
    return jnp.stack([first, second], axis=1).reshape(-1, cols)


def reduce_weight(g):
    rows, cols = g.shape
    fsdp = lax.axis_size("fsdp")
    blocks = g.reshape(fsdp, 2, rows // (2 * fsdp), cols)
    core = lax.axis_index("core")
    mine = lax.dynamic_index_in_dim(blocks, core, axis=1, keepdims=False)
    other = lax.dynamic_index_in_dim(blocks, 1 - core, axis=1, keepdims=False)
    chip = mine + core_swap(other.astype(jnp.bfloat16)).astype(jnp.float32)
    part = lax.psum_scatter(chip.astype(jnp.bfloat16), "fsdp", scatter_dimension=0, tiled=True)
    part = lax.psum(part, ZAX).astype(jnp.float32)
    first, second = in_core_order(part, core_swap(part))
    return jnp.concatenate([first[0], second[0]], axis=0)


def shards(
    block_input,
    key_mask,
    slot_flags,
    norm1_gain,
    norm1_bias,
    qkv_weight,
    query_bias,
    value_bias,
    proj_weight,
    proj_bias,
    norm2_gain,
    norm2_bias,
    up_weight,
    up_bias,
    down_weight,
    down_bias,
    out_grad,
):
    f32, bf16 = (jnp.float32, jnp.bfloat16)
    pairs, part_rows, width = block_input.shape
    group = lax.axis_size("zl") * lax.axis_size("core")
    local_heads = HEADS // group
    slot_len = part_rows * group
    zh = lax.axis_index("zh")
    scale = HEAD ** (-0.5)
    vectors = (
        norm1_gain,
        norm1_bias,
        query_bias,
        value_bias,
        proj_bias,
        norm2_gain,
        norm2_bias,
        up_bias,
        down_bias,
    )
    sizes = [v.shape[0] for v in vectors]
    packed = jnp.concatenate([v.astype(f32) for v in vectors])
    packed = lax.all_gather(packed, "fsdp", axis=0, tiled=False)
    full_vectors = []
    at = 0
    for n in sizes:
        full_vectors.append(packed[:, at : at + n].reshape(-1))
        at += n
    g1, b1, bq, bv, bproj, g2, b2, bup, bdown = full_vectors
    w_qkv = gather_weight(qkv_weight)
    w_proj = gather_weight(proj_weight)
    w_up = gather_weight(up_weight)
    w_down_t = gather_weight(down_weight.T)
    flags = slot_flags.astype(f32).reshape(pairs, 2)
    row_flags = lax.dynamic_index_in_dim(flags, zh, axis=1, keepdims=False)
    live = lax.dynamic_index_in_dim(key_mask.reshape(pairs, 2, -1), zh, axis=1, keepdims=False)
    mask_bias = (live.astype(f32) - 1.0) * 10000.0
    rows = block_input.reshape(pairs * part_rows, width).astype(f32)
    normed, norm_one_back = jax.vjp(layer_norm, rows, g1, b1)
    normed_low = normed.astype(bf16)
    mixed = jnp.dot(normed_low, w_qkv, preferred_element_type=f32)
    q = (mixed[:, :width] + bq).astype(bf16)
    k = mixed[:, width : 2 * width].astype(bf16)
    v = (mixed[:, 2 * width :] + bv).astype(bf16)
    qkv_tok = jnp.stack([q, k, v]).reshape(3, pairs, part_rows, width)
    qkv_heads = lax.all_to_all(qkv_tok, GROUP, split_axis=3, concat_axis=2, tiled=True)
    qkv_heads = qkv_heads.reshape(3, pairs, slot_len, local_heads, HEAD)
    qh, kh, vh = (qkv_heads[0], qkv_heads[1], qkv_heads[2])
    scores = jnp.einsum("pqhd,pkhd->phqk", qh, kh, preferred_element_type=f32) * scale
    shifted = scores + mask_bias[:, None, None, :]
    row_max = jnp.max(shifted, axis=-1, keepdims=True)
    exp_terms = jnp.exp(shifted - row_max)
    probs = exp_terms / jnp.sum(exp_terms, axis=-1, keepdims=True)
    weights_low = probs.astype(bf16)
    attended = jnp.einsum("phqk,pkhd->pqhd", weights_low, vh, preferred_element_type=f32)
    attended = attended.astype(bf16).reshape(pairs, slot_len, local_heads * HEAD)
    merged = lax.all_to_all(attended, GROUP, split_axis=1, concat_axis=2, tiled=True)
    merged_rows = merged.reshape(pairs * part_rows, width)
    hidden = rows + jnp.dot(merged_rows, w_proj, preferred_element_type=f32) + bproj
    second, norm_two_back = jax.vjp(layer_norm, hidden, g2, b2)
    second_low = second.astype(bf16)
    gate_in = jnp.dot(second_low, w_up, preferred_element_type=f32) + bup
    active, gelu_back = jax.vjp(gelu_tanh, gate_in)
    active_low = active.astype(bf16)
    result = (
        hidden
        + lax.dot_general(
            active_low, w_down_t, (((1,), (1,)), ((), ())), preferred_element_type=f32
        )
        + bdown
    )
    row_flag_rows = jnp.repeat(row_flags, part_rows)[:, None]
    output = (result * row_flag_rows).astype(bf16).reshape(pairs, part_rows, width)
    grad_rows = out_grad.reshape(pairs * part_rows, width).astype(f32) * row_flag_rows
    grad_low = grad_rows.astype(bf16)
    down_weight_grad_t = jnp.dot(grad_low.T, active_low, preferred_element_type=f32)
    down_bias_grad = jnp.sum(grad_rows, axis=0)
    grad_active = jnp.dot(grad_low, w_down_t, preferred_element_type=f32)
    grad_gate = gelu_back(grad_active)[0].astype(bf16)
    up_weight_grad = jnp.dot(second_low.T, grad_gate, preferred_element_type=f32)
    up_bias_grad = jnp.sum(grad_gate.astype(f32), axis=0)
    grad_second = jnp.dot(grad_gate, w_up.T, preferred_element_type=f32)
    grad_hidden_norm, norm2_gain_grad, norm2_bias_grad = norm_two_back(grad_second)
    grad_hidden = grad_rows + grad_hidden_norm
    grad_branch = grad_hidden.astype(bf16)
    proj_weight_grad = jnp.dot(merged_rows.T, grad_branch, preferred_element_type=f32)
    proj_bias_grad = jnp.sum(grad_branch.astype(f32), axis=0)
    grad_merged = jnp.dot(grad_branch, w_proj.T, preferred_element_type=f32).astype(bf16)
    grad_heads = lax.all_to_all(
        grad_merged.reshape(pairs, part_rows, width), GROUP, split_axis=2, concat_axis=1, tiled=True
    ).reshape(pairs, slot_len, local_heads, HEAD)
    grad_probs = jnp.einsum("pqhd,pkhd->phqk", grad_heads, vh, preferred_element_type=f32)
    row_dot = jnp.sum(probs * grad_probs, axis=-1, keepdims=True)
    grad_scores = (probs * (grad_probs - row_dot)).astype(bf16)
    dq = (
        jnp.einsum("phqk,pkhd->pqhd", grad_scores, kh, preferred_element_type=f32) * scale
    ).astype(bf16)
    dk = (
        jnp.einsum("phqk,pqhd->pkhd", grad_scores, qh, preferred_element_type=f32) * scale
    ).astype(bf16)
    dv = jnp.einsum("phqk,pqhd->pkhd", weights_low, grad_heads, preferred_element_type=f32).astype(
        bf16
    )
    dqkv = jnp.stack([dq, dk, dv]).reshape(3, pairs, slot_len, local_heads * HEAD)
    dqkv_tok = lax.all_to_all(dqkv, GROUP, split_axis=2, concat_axis=3, tiled=True)
    dqkv_tok = dqkv_tok.reshape(3, pairs * part_rows, width)
    grad_mixed = jnp.concatenate([dqkv_tok[0], dqkv_tok[1], dqkv_tok[2]], axis=1)
    qkv_weight_grad = jnp.dot(normed_low.T, grad_mixed, preferred_element_type=f32)
    query_bias_grad = jnp.sum(dqkv_tok[0].astype(f32), axis=0)
    value_bias_grad = jnp.sum(dqkv_tok[2].astype(f32), axis=0)
    grad_normed = jnp.dot(grad_mixed, w_qkv.T, preferred_element_type=f32)
    grad_rows_norm, norm1_gain_grad, norm1_bias_grad = norm_one_back(grad_normed)
    input_grad = (grad_hidden + grad_rows_norm).reshape(pairs, part_rows, width)
    vec_grads = (
        norm1_gain_grad,
        norm1_bias_grad,
        query_bias_grad,
        value_bias_grad,
        proj_bias_grad,
        norm2_gain_grad,
        norm2_bias_grad,
        up_bias_grad,
        down_bias_grad,
    )
    fsdp = lax.axis_size("fsdp")
    stacked = jnp.concatenate([g.reshape(fsdp, -1) for g in vec_grads], axis=1)
    stacked = lax.psum_scatter(stacked, "fsdp", scatter_dimension=0, tiled=True)
    stacked = lax.psum(stacked, SEQ).reshape(-1)
    vec_out = []
    at = 0
    for g in vec_grads:
        n = g.shape[0] // fsdp
        vec_out.append(stacked[at : at + n])
        at += n
    n1g, n1b, qb, vb, pb, n2g, n2b, ub, db = vec_out
    down_g = reduce_weight(down_weight_grad_t).T
    up_g = reduce_weight(up_weight_grad)
    proj_g = reduce_weight(proj_weight_grad)
    qkv_g = reduce_weight(qkv_weight_grad)
    return (output, input_grad, n1g, n1b, qkv_g, qb, vb, proj_g, pb, n2g, n2b, up_g, ub, down_g, db)


def solution(mesh):
    seq_n = mesh.shape["seq"]
    fsdp_n = mesh.shape["fsdp"]
    devices = mesh.devices.reshape(2, seq_n // 4, 2, fsdp_n)
    inner = Mesh(devices, ("zh", "zl", "core", "fsdp"))
    tok = P("fsdp", SEQ, None)
    vec = P("fsdp")
    rows = P("fsdp", None)
    in_specs = (
        tok,
        rows,
        vec,
        vec,
        vec,
        rows,
        vec,
        vec,
        rows,
        vec,
        vec,
        vec,
        rows,
        vec,
        P(None, "fsdp"),
        vec,
        tok,
    )
    out_specs = (
        tok,
        tok,
        vec,
        vec,
        rows,
        vec,
        vec,
        rows,
        vec,
        vec,
        vec,
        rows,
        vec,
        P(None, "fsdp"),
        vec,
    )
    return jax.shard_map(
        shards, mesh=inner, in_specs=in_specs, out_specs=out_specs, check_vma=False
    )
```

profile of v0, /device:TPU:0, one launch (start us, length us, event | category | flops | bytes accessed | tf_op | source)
XLA Modules:
  0.0 1008.7 jit_solution(17743258620124356132)
XLA Ops:
  14.5 49.5 %all-gather.10.cloned.1.call-done = bf16[576,3456]{1,0:T(8,128)(2,1)} async-done(((bf16[144,3456]{1,0:T(8,128)(2,1)}), bf16[576,3456]{1,0:T(8,128)(2,1)}) %all-gather.10.cloned.1.call-update) | async-done | bytes 3981328 | tf_op jit(solution)/shard_map/all_gather | solution.py:43
  65.6 16.9 %all-reduce = f32[13520]{0:T(1024)S(1)} all-reduce(f32[13520]{0:T(1024)S(1)} %convert_dynamic-update-slice_fusion), channel_id=2, replica_groups=mesh['zh'=2,'zl'=2,'core'=2,'fsdp'=4] {'fsdp'}, use_global_device_ids=true, to_apply=%add | all-reduce | flops 13520 | bytes 108160
  87.9 7.8 all-gather.12.cloned.1.call-done
  95.6 61.8 %all-gather.16.cloned.1.call-done = bf16[576,4304]{1,0:T(8,128)(2,1)} async-done(((bf16[144,4304]{1,0:T(8,128)(2,1)}), bf16[576,4304]{1,0:T(8,128)(2,1)}) %all-gather.16.cloned.1.call-update) | async-done | bytes 4958224 | tf_op jit(solution)/shard_map/all_gather | solution.py:43
  157.5 61.7 %all-gather.14.cloned.1.call-done = bf16[576,4304]{1,0:T(8,128)(2,1)} async-done(((bf16[144,4304]{1,0:T(8,128)(2,1)}), bf16[576,4304]{1,0:T(8,128)(2,1)}) %all-gather.14.cloned.1.call-update) | async-done | bytes 4958224 | tf_op jit(solution)/shard_map/all_gather | solution.py:43
  219.2 5.0 select_bitcast_fusion.5
  224.2 6.1 pad_maximum_fusion.2
  230.2 6.0 fusion.65
  238.7 3.6 copy.88
  242.2 4.1 copy.87
  246.3 4.1 copy.86
  250.5 8.5 pad_maximum_fusion.5
  258.9 4.9 all-to-all-start
  267.6 8.5 select_bitcast_fusion.1
  276.1 8.3 select_bitcast_fusion.3
  284.4 20.6 %all-to-all-done = bf16[3,2,184,1152]{2,1,0,3:T(2,128)(2,1)} async-done(((bf16[3,2,184,1152]{2,1,0,3:T(2,128)(2,1)}), bf16[3,2,184,1152]{2,1,0,3:T(2,128)(2,1)}, u32[]{:S(2)}, u32[]{:S(2)}) %all-to-all-start) | async-done | bytes 2543648 | tf_op jit(solution)/shard_map/all_to_all | solution.py:125
  305.0 12.6 %copy.128 = bf16[3,2,184,4,288]{4,3,2,1,0:T(4,128)(2,1)} copy(bf16[3,2,184,4,288]{2,1,0,4,3:T(2,128)(2,1)} %bitcast.11) | data formatting | bytes 5087232 | tf_op jit(solution)/shard_map/all_to_all | solution.py:125
  317.6 4.5 fusion.60
  332.4 4.1 copy.92
  339.0 10.8 %fusion.63 = (f32[2,4,736]{2,1,0:T(4,128)S(1)}, f32[2,4,736,736]{2,3,1,0:T(8,128)}) fusion(f32[2,736]{1,0:T(2,128)S(1)} %fusion.49, bf16[2,736,4,72]{1,3,2,0:T(8,128)(2,1)} %squeeze.70, bf16[2,736,4,72]{1,3,2,0:T(8,128)(2,1)S(1)} %squeeze.71), kind=kOutput, calls=%fused_computation.161 | convolution fusion | flops 641368768 | bytes 19059456 | tf_op jit(solution)/shard_map/sub | solution.py:131
  349.7 9.1 fusion.34
  358.8 4.7 copy.95
  363.5 4.3 all-to-all-start.1
  367.8 8.7 pad_maximum_fusion
  376.5 8.3 copy.99
  384.8 8.6 pad_maximum_fusion.1
  398.9 3.5 fusion.64
  402.7 8.4 convolution_add_fusion
  411.2 10.9 %convert_reduce_fusion = (f32[4304]{0:T(1024)}, bf16[368,4304]{1,0:T(8,128)(2,1)}) fusion(f32[368,4304]{1,0:T(8,128)S(1)} %convolution_add_fusion, bf16[368,1152]{1,0:T(8,128)(2,1)S(1)} %bitcast.232, bf16[1152,4304]{1,0:T(8,128)(2,1)S(1)} %bitcast.202), kind=kOutput, calls=%fused_computation.32 | convolution fusion | flops 3690417408 | bytes 20284736 | tf_op jit(solution)/shard_map/dot_general | solution.py:157
  422.1 10.1 multiply_reduce_fusion.1
  432.2 10.0 fusion.54
  447.4 4.1 copy.101
  451.6 4.5 all-to-all-start.2
  465.3 6.6 fusion.13
  478.4 12.3 %multiply_reduce_fusion = (f32[2,4,736]{2,1,0:T(4,128)S(1)}, f32[2,4,736,736]{2,3,1,0:T(8,128)}) fusion(f32[2,4,736,736]{2,3,1,0:T(8,128)} %get-tuple-element.83, f32[2,4,736]{2,1,0:T(4,128)S(1)} %get-tuple-element.82, bf16[2,736,4,72]{1,3,2,0:T(8,128)(2,1)} %reshape.304, bf16[2,736,4,72]{1,3,2,0:T(8,128)(2,1)} %squeeze.69), kind=kOutput, calls=%fused_computation.2 | convolution fusion | flops 637028608 | bytes 36411392 | tf_op jit(solution)/shard_map/pqhd,pkhd->phqk/dot_general | solution.py:171
  490.6 12.3 %multiply_convert_fusion = bf16[2,4,736,736]{2,3,1,0:T(8,128)(2,1)S(1)} fusion(f32[2,4,736,736]{2,3,1,0:T(8,128)} %get-tuple-element.88, f32[2,4,736]{2,1,0:T(4,128)S(1)} %get-tuple-element.87, f32[2,4,736,736]{2,3,1,0:T(8,128)} %get-tuple-element.83, f32[2,4,736]{2,1,0:T(4,128)S(1)} %get-tuple-element.82), kind=kLoop, calls=%fused_computation.1 | loop fusion | flops 17334272 | bytes 43382784 | tf_op jit(solution)/shard_map/convert_element_type | solution.py:173
  503.0 9.9 fusion.37
  512.9 3.7 multiply_convert_fusion.2
  519.2 4.7 copy.109
  523.9 4.9 copy.108
  531.6 8.7 pad_maximum_fusion.6
  540.3 4.7 all-to-all-start.3
  545.0 3.5 fusion.26
  548.6 8.7 fusion.3
  559.5 25.1 %all-to-all-done.3 = bf16[3,2,736,288]{3,1,0,2:T(2,128)(2,1)} async-done(((bf16[3,2,736,288]{3,1,0,2:T(2,128)(2,1)}), bf16[3,2,736,288]{3,1,0,2:T(2,128)(2,1)}, u32[]{:S(2)}, u32[]{:S(2)}) %all-to-all-start.3) | async-done | bytes 2543648 | tf_op jit(solution)/shard_map/all_to_all | solution.py:184
  584.6 12.9 %copy.133 = bf16[3,2,4,184,288]{3,2,4,1,0:T(4,128)(2,1)} copy(bf16[3,2,4,184,288]{4,1,0,3,2:T(2,128)(2,1)} %bitcast.47) | data formatting | bytes 5087232 | tf_op jit(solution)/shard_map/all_to_all | solution.py:184
  597.5 4.6 fusion.59
  602.1 4.0 copy.111
  608.9 4.0 copy.112
  622.7 7.4 fusion.66
  634.1 6.1 fusion.27
  640.2 5.5 copy-done.2
  651.7 3.3 fusion.31
  656.8 7.1 fusion.6
  664.0 12.5 %fusion.20 = f32[4,2,144,4304]{3,2,1,0:T(8,128)} fusion(bf16[4,2,144,368]{3,2,1,0:T(8,128)(2,1)S(1)} %bitcast.207, f32[368,4304]{1,0:T(8,128)} %copy-done.13), kind=kOutput, calls=%fused_computation.52 | convolution fusion | flops 3663495936 | bytes 27016192 | tf_op jit(solution)/shard_map/dot_general | solution.py:155
  676.4 4.6 fusion.14
  682.0 8.1 collective-permute-done.10
  690.1 8.9 fusion.2
  699.2 15.0 %reduce-scatter.13.cloned.1.call-done = bf16[1,144,3456]{2,1,0:T(8,128)(2,1)} async-done(((bf16[4,144,3456]{2,1,0:T(8,128)(2,1)}), bf16[1,144,3456]{2,1,0:T(8,128)(2,1)}) %reduce-scatter.13.cloned.1.call-update) | async-done | bytes 995344
  714.2 63.1 %reduce-scatter.19.cloned.1.call-done = bf16[1,144,4304]{2,1,0:T(8,128)(2,1)} async-done(((bf16[4,144,4304]{2,1,0:T(8,128)(2,1)}), bf16[1,144,4304]{2,1,0:T(8,128)(2,1)}) %reduce-scatter.19.cloned.1.call-update) | async-done | bytes 1239568
  777.5 145.8 %all-reduce.9.cloned.1.call-done = (bf16[1,144,3456]{2,1,0:T(8,128)(2,1)}, bf16[1,144,1152]{2,1,0:T(8,128)(2,1)}, bf16[1,144,4304]{2,1,0:T(8,128)(2,1)}, bf16[1,144,4304]{2,1,0:T(8,128)(2,1)}) async-done(((bf16[1,144,3456]{2,1,0:T(8,128)(2,1)}, bf16[1,144,1152]{2,1,0:T(8,128)(2,1)}, bf16[1,144,4304]{2,1,0:T(8,128)(2,1)}, bf16[1,144,4304]{2,1,0:T(8,128)(2,1)}), (bf16[1,144,3456]{2,1,0:T(8,128)(2,1)}, ...) | async-done | bytes 3806224 | tf_op jit(solution)/shard_map/psum | solution.py:58
  926.1 11.2 %fusion.25 = bf16[368,1152]{1,0:T(8,128)(2,1)} fusion(f32[368,1152]{1,0:T(8,128)S(1)} %copy-done.6, bf16[1152,4304]{1,0:T(8,128)(2,1)} %bitcast.199, f32[368]{0:T(512)S(1)} %mul.257, f32[1152]{0:T(1024)S(1)} %add.220, f32[368,4304]{1,0:T(8,128)} %copy-done.13), kind=kOutput, calls=%fused_computation.59 | convolution fusion | flops 3665191680 | bytes 18801600 | tf_op jit(solution)/shard_map/dot_general | solution.py:146
  941.0 17.7 %all-reduce.1 = f32[4,3380]{1,0:T(4,128)} all-reduce(f32[4,3380]{1,0:T(4,128)S(1)} %concatenate.26), channel_id=7, replica_groups=mesh['zh'=2,'zl'=2,'core'=2,'fsdp'=4] {'fsdp'}, use_global_device_ids=true, to_apply=%region_20.21.clone | all-reduce | flops 13520 | bytes 108160
  961.1 27.2 %psum.35 = f32[1,3380]{1,0:T(1,128)S(1)} all-reduce(f32[1,3380]{1,0:T(1,128)S(1)} %constant_dynamic-slice_fusion.5), channel_id=1, replica_groups=mesh['zh'=2,'zl'=2,'core'=2,'fsdp'=4] {'zh','zl','core'}, use_global_device_ids=true, to_apply=%region_21.22 | all-reduce | flops 3380 | bytes 27040 | tf_op jit(solution)/shard_map/psum | solution.py:207
  (268 shorter events, 114.8 us)
Async XLA Ops:
  7.2 56.8 %all-gather.10.cloned.1.call-start = ((), (), s32[]{:S(2)}) async-start(), calls=%async_computation.8 | async-start | bytes 4976640 | tf_op jit(solution)/shard_map/all_gather | solution.py:43
  9.7 85.9 %all-gather.12.cloned.1.call-start = ((), (), s32[]{:S(2)}) async-start(), calls=%async_computation.9 | async-start | bytes 1658880 | tf_op jit(solution)/shard_map/all_gather | solution.py:43
  10.5 146.9 %all-gather.16.cloned.1.call-start = ((), (), s32[]{:S(2)}) async-start(), calls=%async_computation.11 | async-start | bytes 6266880 | tf_op jit(solution)/shard_map/all_gather | solution.py:43
  11.7 52.3 %copy-start.46 = (u32[32]{0:T(128)S(1)}, u32[32]{0:T(128)}, u32[]{:S(2)}) copy-start(u32[32]{0:T(128)} %constant.89) | copy-start | bytes 388
  11.7 53.5 %copy-start.45 = (bf16[1076]{0:T(1024)(128)(2,1)S(1)}, bf16[1076]{0:T(1024)(128)(2,1)}, u32[]{:S(2)}) copy-start(bf16[1076]{0:T(1024)(128)(2,1)} %param.30) | copy-start | bytes 6460
  11.7 53.5 %copy-start.47 = (bf16[288]{0:T(512)(128)(2,1)S(1)}, bf16[288]{0:T(512)(128)(2,1)}, u32[]{:S(2)}) copy-start(bf16[288]{0:T(512)(128)(2,1)} %param.20) | copy-start | bytes 1732
  11.7 53.5 %copy-start.48 = (bf16[288]{0:T(512)(128)(2,1)S(1)}, bf16[288]{0:T(512)(128)(2,1)}, u32[]{:S(2)}) copy-start(bf16[288]{0:T(512)(128)(2,1)} %param.21) | copy-start | bytes 1732
  11.7 53.5 %copy-start.49 = (bf16[288]{0:T(512)(128)(2,1)S(1)}, bf16[288]{0:T(512)(128)(2,1)}, u32[]{:S(2)}) copy-start(bf16[288]{0:T(512)(128)(2,1)} %param.23) | copy-start | bytes 1732
  11.8 53.5 %copy-start.50 = (bf16[288]{0:T(512)(128)(2,1)S(1)}, bf16[288]{0:T(512)(128)(2,1)}, u32[]{:S(2)}) copy-start(bf16[288]{0:T(512)(128)(2,1)} %param.24) | copy-start | bytes 1732
  11.8 53.5 %copy-start.51 = (bf16[288]{0:T(512)(128)(2,1)S(1)}, bf16[288]{0:T(512)(128)(2,1)}, u32[]{:S(2)}) copy-start(bf16[288]{0:T(512)(128)(2,1)} %param.26) | copy-start | bytes 1732
  11.8 53.5 %copy-start.52 = (bf16[288]{0:T(512)(128)(2,1)S(1)}, bf16[288]{0:T(512)(128)(2,1)}, u32[]{:S(2)}) copy-start(bf16[288]{0:T(512)(128)(2,1)} %param.27) | copy-start | bytes 1732
  11.8 53.5 %copy-start.53 = (bf16[288]{0:T(512)(128)(2,1)S(1)}, bf16[288]{0:T(512)(128)(2,1)}, u32[]{:S(2)}) copy-start(bf16[288]{0:T(512)(128)(2,1)} %param.28) | copy-start | bytes 1732
  11.8 53.5 %copy-start.54 = (bf16[288]{0:T(512)(128)(2,1)S(1)}, bf16[288]{0:T(512)(128)(2,1)}, u32[]{:S(2)}) copy-start(bf16[288]{0:T(512)(128)(2,1)} %param.32) | copy-start | bytes 1732
  11.8 71.9 %copy-start.41 = (s32[4,736]{1,0:T(4,128)S(1)}, s32[4,736]{1,0:T(4,128)}, u32[]{:S(2)}) copy-start(s32[4,736]{1,0:T(4,128)} %param.18) | copy-start | bytes 35332
  11.8 71.9 %copy-start.55 = (s32[4]{0:T(128)S(1)}, s32[4]{0:T(128)}, u32[]{:S(2)}) copy-start(s32[4]{0:T(128)} %param.19) | copy-start | bytes 52
  11.8 72.6 %copy-start.3 = (bf16[2,184,1152]{2,1,0:T(8,128)(2,1)S(1)}, bf16[2,184,1152]{2,1,0:T(8,128)(2,1)}, u32[]{:S(2)}) copy-start(bf16[2,184,1152]{2,1,0:T(8,128)(2,1)} %param.17) | copy-start | bytes 2543620
  11.9 73.8 %copy-start.9 = (bf16[2,184,1152]{2,1,0:T(8,128)(2,1)S(1)}, bf16[2,184,1152]{2,1,0:T(8,128)(2,1)}, u32[]{:S(2)}) copy-start(bf16[2,184,1152]{2,1,0:T(8,128)(2,1)} %param.33) | copy-start | bytes 2543620
  11.9 207.3 %all-gather.14.cloned.1.call-start = ((), (), s32[]{:S(2)}) async-start(), calls=%async_computation.10 | async-start | bytes 6266880 | tf_op jit(solution)/shard_map/all_gather | solution.py:43
  64.0 155.2 %collective-permute-start = (bf16[4,144,3456]{2,1,0:T(8,128)(2,1)}, bf16[4,144,3456]{2,1,0:T(8,128)(2,1)}, u32[]{:S(2)}, u32[]{:S(2)}) collective-permute-start(bf16[4,144,3456]{2,1,0:T(8,128)(2,1)} %bitcast.215), channel_id=1, source_target_pairs={{0,4},{4,0},{1,5},{5,1},{2,6},{6,2},{3,7},{7,3},{8,12},{12,8},{9,1... | collective-permute-start | bytes 11943944 | tf_op jit(solution)/shard_map/ppermute | solution.py:31
  84.7 139.5 %copy-start.36 = (f32[2,184]{1,0:T(2,128)}, f32[2,184]{1,0:T(2,128)S(1)}, u32[]{:S(2)}) copy-start(f32[2,184]{1,0:T(2,128)S(1)} %broadcast_multiply_fusion.1) | copy-start | bytes 4420
  95.6 168.2 %collective-permute-start.1 = (bf16[4,144,1152]{2,1,0:T(8,128)(2,1)}, bf16[4,144,1152]{2,1,0:T(8,128)(2,1)}, u32[]{:S(2)}, u32[]{:S(2)}) collective-permute-start(bf16[4,144,1152]{2,1,0:T(8,128)(2,1)} %bitcast.228), channel_id=1, source_target_pairs={{0,4},{4,0},{1,5},{5,1},{2,6},{6,2},{3,7},{7,3},{8,12},{12,8},{9,1... | collective-permute-start | bytes 3981320 | tf_op jit(solution)/shard_map/ppermute | solution.py:31
  157.5 110.1 %collective-permute-start.3 = (bf16[4,144,4304]{2,1,0:T(8,128)(2,1)}, bf16[4,144,4304]{2,1,0:T(8,128)(2,1)}, u32[]{:S(2)}, u32[]{:S(2)}) collective-permute-start(bf16[4,144,4304]{2,1,0:T(8,128)(2,1)} %bitcast.209), channel_id=1, source_target_pairs={{0,4},{4,0},{1,5},{5,1},{2,6},{6,2},{3,7},{7,3},{8,12},{12,8},{9,1... | collective-permute-start | bytes 14874632 | tf_op jit(solution)/shard_map/ppermute | solution.py:31
  219.2 56.9 %collective-permute-start.2 = (bf16[4,144,4304]{2,1,0:T(8,128)(2,1)}, bf16[4,144,4304]{2,1,0:T(8,128)(2,1)}, u32[]{:S(2)}, u32[]{:S(2)}) collective-permute-start(bf16[4,144,4304]{2,1,0:T(8,128)(2,1)} %bitcast.211), channel_id=1, source_target_pairs={{0,4},{4,0},{1,5},{5,1},{2,6},{6,2},{3,7},{7,3},{8,12},{12,8},{9,1... | collective-permute-start | bytes 14874632 | tf_op jit(solution)/shard_map/ppermute | solution.py:31
  258.9 46.0 %all-to-all-start = ((bf16[3,2,184,1152]{2,1,0,3:T(2,128)(2,1)}), bf16[3,2,184,1152]{2,1,0,3:T(2,128)(2,1)}, u32[]{:S(2)}, u32[]{:S(2)}) async-start(bf16[3,2,184,1152]{2,1,0,3:T(2,128)(2,1)} %pad_maximum_fusion.5), calls=%async_computation | async-start | bytes 7077888 | tf_op jit(solution)/shard_map/all_to_all | solution.py:125
  363.5 29.9 %all-to-all-start.1 = ((bf16[2,736,288]{2,0,1:T(2,128)(2,1)}), bf16[2,736,288]{2,0,1:T(2,128)(2,1)}, u32[]{:S(2)}, u32[]{:S(2)}) async-start(bf16[2,736,288]{2,0,1:T(2,128)(2,1)} %copy.95), calls=%async_computation.1 | async-start | bytes 2260992 | tf_op jit(solution)/shard_map/all_to_all | solution.py:136
  402.3 39.8 %copy-start.5 = (f32[368,1152]{1,0:T(8,128)}, f32[368,1152]{1,0:T(8,128)S(1)}, u32[]{:S(2)}) copy-start(f32[368,1152]{1,0:T(8,128)S(1)} %get-tuple-element.85) | copy-start | bytes 5087236
  402.4 8.8 slice-start
  402.7 8.5 slice-start.1
  402.7 8.5 slice-start.2
  402.7 8.5 copy-start.29
  411.1 11.0 %copy-start.13 = (f32[368,4304]{1,0:T(8,128)}, f32[368,4304]{1,0:T(8,128)S(1)}, u32[]{:S(2)}) copy-start(f32[368,4304]{1,0:T(8,128)S(1)} %convolution_add_fusion) | copy-start | bytes 19006468
  422.1 10.1 copy-start.25
  451.6 20.4 %all-to-all-start.2 = ((bf16[2,184,1152]{1,0,2:T(2,128)(2,1)}), bf16[2,184,1152]{1,0,2:T(2,128)(2,1)}, u32[]{:S(2)}, u32[]{:S(2)}) async-start(bf16[2,184,1152]{1,0,2:T(2,128)(2,1)} %copy.101), calls=%async_computation.2 | async-start | bytes 2359296 | tf_op jit(solution)/shard_map/all_to_all | solution.py:168
  464.8 80.3 %collective-permute-start.6 = (bf16[4,144,1152]{2,1,0:T(8,128)(2,1)}, bf16[4,144,1152]{2,1,0:T(8,128)(2,1)}, u32[]{:S(2)}, u32[]{:S(2)}) collective-permute-start(bf16[4,144,1152]{2,1,0:T(8,128)(2,1)} %fusion.40), channel_id=1, source_target_pairs={{0,4},{4,0},{1,5},{5,1},{2,6},{6,2},{3,7},{7,3},{8,12},{12,8},{9,1... | collective-permute-start | bytes 3981320 | tf_op jit(solution)/shard_map/ppermute | solution.py:31
  471.9 76.7 %collective-permute-start.8 = (bf16[4,144,4304]{2,1,0:T(8,128)(2,1)}, bf16[4,144,4304]{2,1,0:T(8,128)(2,1)}, u32[]{:S(2)}, u32[]{:S(2)}) collective-permute-start(bf16[4,144,4304]{2,1,0:T(8,128)(2,1)} %fusion.13), channel_id=1, source_target_pairs={{0,4},{4,0},{1,5},{5,1},{2,6},{6,2},{3,7},{7,3},{8,12},{12,8},{9,1... | collective-permute-start | bytes 14874632 | tf_op jit(solution)/shard_map/ppermute | solution.py:31
  490.6 12.3 %copy-start.28 = (bf16[2,736,4,72]{1,3,2,0:T(8,128)(2,1)S(1)}, bf16[2,736,4,72]{1,3,2,0:T(8,128)(2,1)}, u32[]{:S(2)}) copy-start(bf16[2,736,4,72]{1,3,2,0:T(8,128)(2,1)} %reshape.304) | copy-start | bytes 2543620
  503.0 9.9 copy-start.21
  519.2 9.6 copy-start.14
  540.3 44.3 %all-to-all-start.3 = ((bf16[3,2,736,288]{3,1,0,2:T(2,128)(2,1)}), bf16[3,2,736,288]{3,1,0,2:T(2,128)(2,1)}, u32[]{:S(2)}, u32[]{:S(2)}) async-start(bf16[3,2,736,288]{3,1,0,2:T(2,128)(2,1)} %pad_maximum_fusion.6), calls=%async_computation.3 | async-start | bytes 6782976 | tf_op jit(solution)/shard_map/all_to_all | solution.py:184
  545.0 154.2 %reduce-scatter.15.cloned.1.call-start = ((), (), s32[]{:S(2)}) async-start(), calls=%async_computation.13 | async-start | bytes 1658880
  548.5 150.7 %reduce-scatter.17.cloned.1.call-start = ((), (), s32[]{:S(2)}) async-start(), calls=%async_computation.14 | async-start | bytes 6266880
  557.3 156.9 %reduce-scatter.13.cloned.1.call-start = ((), (), s32[]{:S(2)}) async-start(), calls=%async_computation.12 | async-start | bytes 4976640
  622.7 7.5 copy-start.19
  622.7 7.5 copy-start.10
  622.7 7.5 copy-start.32
  622.7 7.5 copy-start.34
  648.1 8.7 collective-permute-start.4
  663.9 113.4 %reduce-scatter.19.cloned.1.call-start = ((), (), s32[]{:S(2)}) async-start(), calls=%async_computation.15 | async-start | bytes 6266880
  681.0 9.1 collective-permute-start.10
  698.9 78.4 %copy-start.39 = (f32[4,288]{1,0:T(4,128)S(1)}, f32[4,288]{1,0:T(4,128)}, u32[]{:S(2)}) copy-start(f32[4,288]{1,0:T(4,128)} %get-tuple-element.71) | copy-start | bytes 13828
  699.0 78.5 %copy-start.35 = (f32[1152]{0:T(1024)S(1)}, f32[1152]{0:T(1024)}, u32[]{:S(2)}) copy-start(f32[1152]{0:T(1024)} %get-tuple-element.68) | copy-start | bytes 13828
  699.0 224.4 %all-reduce.9.cloned.1.call-start = ((), (), s32[]{:S(2)}) async-start(), calls=%async_computation.16 | async-start | bytes 7667712 | tf_op jit(solution)/shard_map/psum | solution.py:58
  777.3 148.7 %copy-start.6 = (f32[368,1152]{1,0:T(8,128)S(1)}, f32[368,1152]{1,0:T(8,128)}, u32[]{:S(2)}) copy-start(f32[368,1152]{1,0:T(8,128)} %copy-done.5) | copy-start | bytes 5087236
  926.0 11.3 %copy-start.38 = (f32[1152]{0:T(1024)S(1)}, f32[1152]{0:T(1024)}, u32[]{:S(2)}) copy-start(f32[1152]{0:T(1024)} %get-tuple-element.37) | copy-start | bytes 13828
  926.0 11.3 %copy-start.43 = (f32[1152]{0:T(1024)S(1)}, f32[1152]{0:T(1024)}, u32[]{:S(2)}) copy-start(f32[1152]{0:T(1024)} %get-tuple-element.17) | copy-start | bytes 13828
  926.0 11.4 %copy-start.42 = (f32[1152]{0:T(1024)S(1)}, f32[1152]{0:T(1024)}, u32[]{:S(2)}) copy-start(f32[1152]{0:T(1024)} %get-tuple-element.19) | copy-start | bytes 13828
  926.0 11.5 %copy-start.40 = (f32[4304]{0:T(1024)S(1)}, f32[4304]{0:T(1024)}, u32[]{:S(2)}) copy-start(f32[4304]{0:T(1024)} %get-tuple-element.35) | copy-start | bytes 51652
  926.0 65.9 %collective-permute-start.5 = (f32[1,144,3456]{2,1,0:T(8,128)}, f32[1,144,3456]{2,1,0:T(8,128)}, u32[]{:S(2)}, u32[]{:S(2)}) collective-permute-start(f32[1,144,3456]{2,1,0:T(8,128)} %convert_element_type.225), channel_id=1, source_target_pairs={{0,4},{4,0},{1,5},{5,1},{2,6},{6,2},{3,7},{7,3},{8,12},{12,8},{9,1... | collective-permute-start | bytes 5971976 | tf_op jit(solution)/shard_map/ppermute | solution.py:31
  937.2 21.5 %copy-start.27 = (bf16[1,144,1152]{2,1,0:T(8,128)(2,1)S(1)}, bf16[1,144,1152]{2,1,0:T(8,128)(2,1)}, u32[]{:S(2)}) copy-start(bf16[1,144,1152]{2,1,0:T(8,128)(2,1)} %get-tuple-element.32) | copy-start | bytes 995332
  937.2 52.4 %copy-start.17 = (bf16[1,144,4304]{2,1,0:T(8,128)(2,1)S(1)}, bf16[1,144,4304]{2,1,0:T(8,128)(2,1)}, u32[]{:S(2)}) copy-start(bf16[1,144,4304]{2,1,0:T(8,128)(2,1)} %get-tuple-element.33) | copy-start | bytes 3718660
  940.7 49.2 %copy-start.15 = (bf16[1,144,4304]{2,1,0:T(8,128)(2,1)S(1)}, bf16[1,144,4304]{2,1,0:T(8,128)(2,1)}, u32[]{:S(2)}) copy-start(bf16[1,144,4304]{2,1,0:T(8,128)(2,1)} %get-tuple-element.34) | copy-start | bytes 3718660
  959.6 31.0 %collective-permute-start.7 = (f32[1,144,1152]{2,1,0:T(8,128)}, f32[1,144,1152]{2,1,0:T(8,128)S(1)}, u32[]{:S(2)}, u32[]{:S(2)}) collective-permute-start(f32[1,144,1152]{2,1,0:T(8,128)} %convert_element_type.230), channel_id=1, source_target_pairs={{0,4},{4,0},{1,5},{5,1},{2,6},{6,2},{3,7},{7,3},{8,12},{12,8},{9,1... | collective-permute-start | bytes 1990664 | tf_op jit(solution)/shard_map/ppermute | solution.py:31
  989.8 6.1 collective-permute-start.9
  990.1 8.8 collective-permute-start.11
  (20 other events, 51.0 us)
Sparse Core Ops, SparseCore 0:
  10.4 53.5 all-gather.9
  66.4 29.1 all-gather.11
  98.1 59.3 all-gather.15
  159.7 59.3 all-gather.13
  549.1 30.4 reduce-scatter.14
  583.1 59.4 reduce-scatter.16
  664.0 50.1 reduce-scatter.12
  717.8 59.4 reduce-scatter.18
  780.0 143.3 all-reduce.8
where the time goes:
time: 1020 us; the launch traced here: 1010 us
  waiting for transfers between devices  459 us (45%)
  local copies, waits for them, and re-layouts  171 us (17%)
  other arithmetic  141 us (14%)
  matrix products  140 us (14%)
  blocking collectives  61.8 us (6%)
  starting transfers between devices  21.1 us (2%)
  between operations  15.7 us (2%)
    all_gather x4, waiting for transfers between devices, gather_weight(): mine = lax.all_gather(piece, 'fsdp', axis=0, tiled=False)  181 us
    psum x1, waiting for transfers between devices, reduce_weight(): part = lax.psum(part, ZAX).astype(jnp.float32)  146 us
    unnamed x13, waiting for transfers between devices  78.3 us
    another operation x8, other arithmetic, gather_weight(): return jnp.stack([first, second], axis=1).reshape(-1, cols)  48.9 us
    unnamed x2, blocking collectives  34.6 us
    convert_element_type x4, other arithmetic, reduce_weight(): chip.astype(jnp.bfloat16)  28.1 us
    psum x1, blocking collectives, shards(): stacked = lax.psum(stacked, SEQ).reshape(-1)  27.2 us
    all_to_all x1, waiting for transfers between devices, shards(): lax.all_to_all(dqkv, GROUP, split_axis=2, concat_axis=3, tiled=True)  25.1 us
  transfers between devices with their start and end apart: 25, of which 10 were waited for; matrix products, arithmetic and copies ran while one was open for 32% of the time, Pallas kernels for 0%

commit v1 on v0

--- a/solution.py
+++ b/solution.py
@@ -122,7 +122,10 @@
     k = mixed[:, width : 2 * width].astype(bf16)
     v = (mixed[:, 2 * width :] + bv).astype(bf16)
     qkv_tok = jnp.stack([q, k, v]).reshape(3, pairs, part_rows, width)
-    qkv_heads = lax.all_to_all(qkv_tok, GROUP, split_axis=3, concat_axis=2, tiled=True)
+    qkv_heads = jnp.concatenate(
+        lax.all_to_all(jnp.stack(jnp.split(qkv_tok, lax.axis_size(GROUP), axis=3)), GROUP, 0, 0),
+        axis=2,
+    )
     qkv_heads = qkv_heads.reshape(3, pairs, slot_len, local_heads, HEAD)
     qh, kh, vh = (qkv_heads[0], qkv_heads[1], qkv_heads[2])
     scores = jnp.einsum("pqhd,pkhd->phqk", qh, kh, preferred_element_type=f32) * scale

time: 1020 us -> 983 us (0.964)
  local copies, waits for them, and re-layouts: 171 us -> 145 us
    all_to_all x1 -> x0, local copies, waits for them, and re-layouts: 12.6 us -> none  [shards(): lax.all_to_all(qkv_tok, GROUP, split_axis=3, concat_axis=2, tiled=True)]
    another operation x3 -> x1, local copies, waits for them, and re-layouts: 11.8 us -> 1.42 us  [shards(): jnp.stack(jnp.split(qkv_tok, lax.axis_size(GROUP), axis=3))]
  transfers between devices with their start and end apart: 25 -> 25, of which waited for: 10 -> 10; matrix products, arithmetic and copies ran while one was open for 32% -> 31% of each run, Pallas kernels for 0% -> 0%
where the time goes in v1:
time: 983 us; the launch traced here: 974 us
  waiting for transfers between devices  457 us (46%)
  local copies, waits for them, and re-layouts  145 us (15%)
  matrix products  140 us (14%)
  other arithmetic  134 us (14%)
  blocking collectives  61.8 us (6%)
  starting transfers between devices  21.2 us (2%)
  between operations  15.7 us (2%)
    all_gather x4, waiting for transfers between devices, gather_weight(): mine = lax.all_gather(piece, 'fsdp', axis=0, tiled=False)  181 us
    psum x1, waiting for transfers between devices, reduce_weight(): part = lax.psum(part, ZAX).astype(jnp.float32)  146 us
    unnamed x13, waiting for transfers between devices  78.2 us
    another operation x8, other arithmetic, gather_weight(): return jnp.stack([first, second], axis=1).reshape(-1, cols)  48.9 us
    unnamed x2, blocking collectives  34.6 us
    convert_element_type x4, other arithmetic, reduce_weight(): chip.astype(jnp.bfloat16)  28.1 us
    psum x1, blocking collectives, shards(): stacked = lax.psum(stacked, SEQ).reshape(-1)  27.2 us
    all_to_all x1, waiting for transfers between devices, shards(): lax.all_to_all(dqkv, GROUP, split_axis=2, concat_axis=3, tiled=True)  25.1 us
  transfers between devices with their start and end apart: 25, of which 10 were waited for; matrix products, arithmetic and copies ran while one was open for 31% of the time, Pallas kernels for 0%

profile of v1, /device:TPU:0, one launch (start us, length us, event | category | flops | bytes accessed | tf_op | source)
XLA Modules:
  0.0 973.8 jit_solution(10636451179020538937)
XLA Ops:
  14.5 49.5 %all-gather.10.cloned.1.call-done = bf16[576,3456]{1,0:T(8,128)(2,1)} async-done(((bf16[144,3456]{1,0:T(8,128)(2,1)}), bf16[576,3456]{1,0:T(8,128)(2,1)}) %all-gather.10.cloned.1.call-update) | async-done | bytes 3981328 | tf_op jit(solution)/shard_map/all_gather | solution.py:43
  65.6 16.9 %all-reduce = f32[13520]{0:T(1024)S(1)} all-reduce(f32[13520]{0:T(1024)S(1)} %convert_dynamic-update-slice_fusion), channel_id=2, replica_groups=mesh['zh'=2,'zl'=2,'core'=2,'fsdp'=4] {'fsdp'}, use_global_device_ids=true, to_apply=%add | all-reduce | flops 13520 | bytes 108160
  87.8 7.8 all-gather.12.cloned.1.call-done
  95.6 61.8 %all-gather.16.cloned.1.call-done = bf16[576,4304]{1,0:T(8,128)(2,1)} async-done(((bf16[144,4304]{1,0:T(8,128)(2,1)}), bf16[576,4304]{1,0:T(8,128)(2,1)}) %all-gather.16.cloned.1.call-update) | async-done | bytes 4958224 | tf_op jit(solution)/shard_map/all_gather | solution.py:43
  157.5 61.7 %all-gather.14.cloned.1.call-done = bf16[576,4304]{1,0:T(8,128)(2,1)} async-done(((bf16[144,4304]{1,0:T(8,128)(2,1)}), bf16[576,4304]{1,0:T(8,128)(2,1)}) %all-gather.14.cloned.1.call-update) | async-done | bytes 4958224 | tf_op jit(solution)/shard_map/all_gather | solution.py:43
  219.2 5.0 select_bitcast_fusion.5
  224.2 6.0 pad_maximum_fusion.2
  230.2 6.0 fusion.65
  240.5 4.9 all-to-all-start
  249.2 8.5 select_bitcast_fusion.1
  257.7 8.3 select_bitcast_fusion.3
  266.0 19.0 %all-to-all-done = bf16[4,3,2,184,288]{4,3,2,1,0:T(8,128)(2,1)} async-done(((bf16[4,3,2,184,288]{4,3,2,1,0:T(8,128)(2,1)}), bf16[4,3,2,184,288]{4,3,2,1,0:T(8,128)(2,1)}, u32[]{:S(2)}, u32[]{:S(2)}) %all-to-all-start) | async-done | bytes 2543648 | tf_op jit(solution)/shard_map/all_to_all | solution.py:126
  285.0 3.8 fusion.60
  298.1 3.4 copy.96
  304.0 10.6 %fusion.63 = (f32[2,4,736]{2,1,0:T(4,128)S(1)}, f32[2,4,736,736]{2,3,1,0:T(8,128)}) fusion(f32[2,736]{1,0:T(2,128)S(1)} %fusion.49, bf16[2,736,4,72]{1,3,2,0:T(8,128)(2,1)} %squeeze.70, bf16[2,736,4,72]{1,3,2,0:T(8,128)(2,1)S(1)} %squeeze.71), kind=kOutput, calls=%fused_computation.166 | convolution fusion | flops 641368768 | bytes 19059456 | tf_op jit(solution)/shard_map/sub | solution.py:134
  314.5 9.1 fusion.34
  323.6 4.7 copy.99
  328.2 4.5 all-to-all-start.1
  332.7 8.7 pad_maximum_fusion
  341.4 8.3 copy.103
  349.8 8.6 pad_maximum_fusion.1
  363.9 3.5 fusion.64
  367.7 8.4 convolution_add_fusion
  376.2 10.9 %convert_reduce_fusion = (f32[4304]{0:T(1024)}, bf16[368,4304]{1,0:T(8,128)(2,1)}) fusion(f32[368,4304]{1,0:T(8,128)S(1)} %convolution_add_fusion, bf16[368,1152]{1,0:T(8,128)(2,1)S(1)} %bitcast.238, bf16[1152,4304]{1,0:T(8,128)(2,1)S(1)} %bitcast.208), kind=kOutput, calls=%fused_computation.32 | convolution fusion | flops 3690417408 | bytes 20284736 | tf_op jit(solution)/shard_map/dot_general | solution.py:160
  387.1 10.1 %multiply_reduce_fusion.1 = (f32[1152]{0:T(1024)}, f32[368]{0:T(512)S(1)}, f32[1152]{0:T(1024)}, f32[368,1152]{1,0:T(8,128)S(1)}) fusion(f32[368,1152]{1,0:T(8,128)S(1)} %get-tuple-element.89, f32[368]{0:T(512)S(1)} %fusion.50, f32[368]{0:T(512)S(1)} %broadcast_multiply_fusion, f32[1152]{0:T(1024)S(1)} %mul.248, bf16[368,4304]{1,0:T(8,128)(2,1)} %get-tuple-element.36, ...), kind=kOutput, calls=%fused_computation.88 | convolution fusion | flops 3652630016 | bytes 16493888 | tf_op jit(solution)/shard_map/dot_general | solution.py:164
  397.2 9.9 %fusion.54 = f32[1152,4304]{1,0:T(8,128)} fusion(bf16[368,4304]{1,0:T(8,128)(2,1)S(1)} %copy-done.25, f32[368,1152]{1,0:T(8,128)S(1)} %get-tuple-element.89, f32[1152]{0:T(1024)S(1)} %add.211, f32[1152]{0:T(1024)S(1)} %mul.248, f32[368]{0:T(512)S(1)} %fusion.50, f32[368]{0:T(512)S(1)} %broadcast_multiply_fusion), kind=kOutput, calls=%fused_computation.159 | convolution fusion | flops 3651360768 | bytes 24708480 | tf_op jit(solution)/shard_map/dot_general | solution.py:162
  412.4 4.1 copy.105
  416.5 4.5 all-to-all-start.2
  423.2 3.0 fusion.43
  430.2 6.6 fusion.13
  436.9 3.2 copy.147
  440.1 3.2 reshape.306
  443.3 12.3 %multiply_reduce_fusion = (f32[2,4,736]{2,1,0:T(4,128)S(1)}, f32[2,4,736,736]{2,3,1,0:T(8,128)}) fusion(f32[2,4,736,736]{2,3,1,0:T(8,128)} %get-tuple-element.87, f32[2,4,736]{2,1,0:T(4,128)S(1)} %get-tuple-element.86, bf16[2,736,4,72]{1,3,2,0:T(8,128)(2,1)} %reshape.306, bf16[2,736,4,72]{1,3,2,0:T(8,128)(2,1)} %squeeze.69), kind=kOutput, calls=%fused_computation.2 | convolution fusion | flops 637028608 | bytes 36411392 | tf_op jit(solution)/shard_map/pqhd,pkhd->phqk/dot_general | solution.py:174
  455.6 12.3 %multiply_convert_fusion = bf16[2,4,736,736]{2,3,1,0:T(8,128)(2,1)S(1)} fusion(f32[2,4,736,736]{2,3,1,0:T(8,128)} %get-tuple-element.92, f32[2,4,736]{2,1,0:T(4,128)S(1)} %get-tuple-element.91, f32[2,4,736,736]{2,3,1,0:T(8,128)} %get-tuple-element.87, f32[2,4,736]{2,1,0:T(4,128)S(1)} %get-tuple-element.86), kind=kLoop, calls=%fused_computation.1 | loop fusion | flops 17334272 | bytes 43382784 | tf_op jit(solution)/shard_map/convert_element_type | solution.py:176
  467.9 9.9 %fusion.37 = bf16[2,4,72,736]{3,2,1,0:T(8,128)(2,1)} fusion(bf16[2,736,4,72]{1,3,2,0:T(8,128)(2,1)S(1)} %copy-done.28, f32[2,4,736,736]{2,3,1,0:T(8,128)} %get-tuple-element.87, f32[2,4,736]{2,1,0:T(4,128)S(1)} %get-tuple-element.86), kind=kOutput, calls=%fused_computation.105 | convolution fusion | flops 633124864 | bytes 19053568 | tf_op jit(solution)/shard_map/phqk,pqhd->pkhd/dot_general | solution.py:183
  477.9 3.7 multiply_convert_fusion.2
  484.2 4.7 copy.113
  488.9 4.9 copy.112
  496.6 8.7 pad_maximum_fusion.6
  505.3 4.7 all-to-all-start.3
  510.0 3.5 fusion.26
  513.6 8.7 fusion.3
  524.5 25.1 %all-to-all-done.3 = bf16[3,2,736,288]{3,1,0,2:T(2,128)(2,1)} async-done(((bf16[3,2,736,288]{3,1,0,2:T(2,128)(2,1)}), bf16[3,2,736,288]{3,1,0,2:T(2,128)(2,1)}, u32[]{:S(2)}, u32[]{:S(2)}) %all-to-all-start.3) | async-done | bytes 2543648 | tf_op jit(solution)/shard_map/all_to_all | solution.py:187
  549.6 12.9 %copy.136 = bf16[3,2,4,184,288]{3,2,4,1,0:T(4,128)(2,1)} copy(bf16[3,2,4,184,288]{4,1,0,3,2:T(2,128)(2,1)} %bitcast.50) | data formatting | bytes 5087232 | tf_op jit(solution)/shard_map/all_to_all | solution.py:187
  562.5 4.6 fusion.59
  567.1 4.0 copy.115
  571.1 2.9 squeeze.73
  574.0 4.0 copy.116
  583.3 2.9 squeeze.75
  587.7 7.5 fusion.66
  599.2 6.1 fusion.27
  605.3 5.5 copy-done.2
  616.8 3.3 fusion.31
  621.9 7.1 fusion.6
  629.1 12.5 %fusion.20 = f32[4,2,144,4304]{3,2,1,0:T(8,128)} fusion(bf16[4,2,144,368]{3,2,1,0:T(8,128)(2,1)S(1)} %bitcast.213, f32[368,4304]{1,0:T(8,128)} %copy-done.13), kind=kOutput, calls=%fused_computation.52 | convolution fusion | flops 3663495936 | bytes 27016192 | tf_op jit(solution)/shard_map/dot_general | solution.py:158
  641.5 4.6 fusion.14
  647.1 8.1 collective-permute-done.10
  655.1 8.9 fusion.2
  664.3 15.0 %reduce-scatter.13.cloned.1.call-done = bf16[1,144,3456]{2,1,0:T(8,128)(2,1)} async-done(((bf16[4,144,3456]{2,1,0:T(8,128)(2,1)}), bf16[1,144,3456]{2,1,0:T(8,128)(2,1)}) %reduce-scatter.13.cloned.1.call-update) | async-done | bytes 995344
  679.3 63.1 %reduce-scatter.19.cloned.1.call-done = bf16[1,144,4304]{2,1,0:T(8,128)(2,1)} async-done(((bf16[4,144,4304]{2,1,0:T(8,128)(2,1)}), bf16[1,144,4304]{2,1,0:T(8,128)(2,1)}) %reduce-scatter.19.cloned.1.call-update) | async-done | bytes 1239568
  742.6 145.8 %all-reduce.9.cloned.1.call-done = (bf16[1,144,3456]{2,1,0:T(8,128)(2,1)}, bf16[1,144,1152]{2,1,0:T(8,128)(2,1)}, bf16[1,144,4304]{2,1,0:T(8,128)(2,1)}, bf16[1,144,4304]{2,1,0:T(8,128)(2,1)}) async-done(((bf16[1,144,3456]{2,1,0:T(8,128)(2,1)}, bf16[1,144,1152]{2,1,0:T(8,128)(2,1)}, bf16[1,144,4304]{2,1,0:T(8,128)(2,1)}, bf16[1,144,4304]{2,1,0:T(8,128)(2,1)}), (bf16[1,144,3456]{2,1,0:T(8,128)(2,1)}, ...) | async-done | bytes 3806224 | tf_op jit(solution)/shard_map/psum | solution.py:58
  891.2 11.2 %fusion.25 = bf16[368,1152]{1,0:T(8,128)(2,1)} fusion(f32[368,1152]{1,0:T(8,128)S(1)} %copy-done.6, bf16[1152,4304]{1,0:T(8,128)(2,1)} %bitcast.205, f32[368]{0:T(512)S(1)} %mul.257, f32[1152]{0:T(1024)S(1)} %add.220, f32[368,4304]{1,0:T(8,128)} %copy-done.13), kind=kOutput, calls=%fused_computation.59 | convolution fusion | flops 3665191680 | bytes 18801600 | tf_op jit(solution)/shard_map/dot_general | solution.py:149
  906.0 17.7 %all-reduce.1 = f32[4,3380]{1,0:T(4,128)} all-reduce(f32[4,3380]{1,0:T(4,128)S(1)} %concatenate.26), channel_id=7, replica_groups=mesh['zh'=2,'zl'=2,'core'=2,'fsdp'=4] {'fsdp'}, use_global_device_ids=true, to_apply=%region_20.21.clone | all-reduce | flops 13520 | bytes 108160
  926.1 27.2 %psum.35 = f32[1,3380]{1,0:T(1,128)S(1)} all-reduce(f32[1,3380]{1,0:T(1,128)S(1)} %constant_dynamic-slice_fusion.5), channel_id=1, replica_groups=mesh['zh'=2,'zl'=2,'core'=2,'fsdp'=4] {'zh','zl','core'}, use_global_device_ids=true, to_apply=%region_21.22 | all-reduce | flops 3380 | bytes 27040 | tf_op jit(solution)/shard_map/psum | solution.py:210
  (266 shorter events, 100.4 us)
Async XLA Ops:
  7.2 56.8 %all-gather.10.cloned.1.call-start = ((), (), s32[]{:S(2)}) async-start(), calls=%async_computation.8 | async-start | bytes 4976640 | tf_op jit(solution)/shard_map/all_gather | solution.py:43
  9.7 85.9 %all-gather.12.cloned.1.call-start = ((), (), s32[]{:S(2)}) async-start(), calls=%async_computation.9 | async-start | bytes 1658880 | tf_op jit(solution)/shard_map/all_gather | solution.py:43
  10.5 146.9 %all-gather.16.cloned.1.call-start = ((), (), s32[]{:S(2)}) async-start(), calls=%async_computation.11 | async-start | bytes 6266880 | tf_op jit(solution)/shard_map/all_gather | solution.py:43
  11.7 52.3 %copy-start.46 = (u32[32]{0:T(128)S(1)}, u32[32]{0:T(128)}, u32[]{:S(2)}) copy-start(u32[32]{0:T(128)} %constant.89) | copy-start | bytes 388
  11.7 53.5 %copy-start.45 = (bf16[1076]{0:T(1024)(128)(2,1)S(1)}, bf16[1076]{0:T(1024)(128)(2,1)}, u32[]{:S(2)}) copy-start(bf16[1076]{0:T(1024)(128)(2,1)} %param.30) | copy-start | bytes 6460
  11.7 53.5 %copy-start.47 = (bf16[288]{0:T(512)(128)(2,1)S(1)}, bf16[288]{0:T(512)(128)(2,1)}, u32[]{:S(2)}) copy-start(bf16[288]{0:T(512)(128)(2,1)} %param.20) | copy-start | bytes 1732
  11.7 53.5 %copy-start.48 = (bf16[288]{0:T(512)(128)(2,1)S(1)}, bf16[288]{0:T(512)(128)(2,1)}, u32[]{:S(2)}) copy-start(bf16[288]{0:T(512)(128)(2,1)} %param.21) | copy-start | bytes 1732
  11.7 53.5 %copy-start.49 = (bf16[288]{0:T(512)(128)(2,1)S(1)}, bf16[288]{0:T(512)(128)(2,1)}, u32[]{:S(2)}) copy-start(bf16[288]{0:T(512)(128)(2,1)} %param.23) | copy-start | bytes 1732
  11.8 53.5 %copy-start.50 = (bf16[288]{0:T(512)(128)(2,1)S(1)}, bf16[288]{0:T(512)(128)(2,1)}, u32[]{:S(2)}) copy-start(bf16[288]{0:T(512)(128)(2,1)} %param.24) | copy-start | bytes 1732
  11.8 53.5 %copy-start.51 = (bf16[288]{0:T(512)(128)(2,1)S(1)}, bf16[288]{0:T(512)(128)(2,1)}, u32[]{:S(2)}) copy-start(bf16[288]{0:T(512)(128)(2,1)} %param.26) | copy-start | bytes 1732
  11.8 53.5 %copy-start.52 = (bf16[288]{0:T(512)(128)(2,1)S(1)}, bf16[288]{0:T(512)(128)(2,1)}, u32[]{:S(2)}) copy-start(bf16[288]{0:T(512)(128)(2,1)} %param.27) | copy-start | bytes 1732
  11.8 53.5 %copy-start.53 = (bf16[288]{0:T(512)(128)(2,1)S(1)}, bf16[288]{0:T(512)(128)(2,1)}, u32[]{:S(2)}) copy-start(bf16[288]{0:T(512)(128)(2,1)} %param.28) | copy-start | bytes 1732
  11.8 53.5 %copy-start.54 = (bf16[288]{0:T(512)(128)(2,1)S(1)}, bf16[288]{0:T(512)(128)(2,1)}, u32[]{:S(2)}) copy-start(bf16[288]{0:T(512)(128)(2,1)} %param.32) | copy-start | bytes 1732
  11.8 71.9 %copy-start.41 = (s32[4,736]{1,0:T(4,128)S(1)}, s32[4,736]{1,0:T(4,128)}, u32[]{:S(2)}) copy-start(s32[4,736]{1,0:T(4,128)} %param.18) | copy-start | bytes 35332
  11.8 71.9 %copy-start.55 = (s32[4]{0:T(128)S(1)}, s32[4]{0:T(128)}, u32[]{:S(2)}) copy-start(s32[4]{0:T(128)} %param.19) | copy-start | bytes 52
  11.8 72.6 %copy-start.3 = (bf16[2,184,1152]{2,1,0:T(8,128)(2,1)S(1)}, bf16[2,184,1152]{2,1,0:T(8,128)(2,1)}, u32[]{:S(2)}) copy-start(bf16[2,184,1152]{2,1,0:T(8,128)(2,1)} %param.17) | copy-start | bytes 2543620
  11.9 73.8 %copy-start.9 = (bf16[2,184,1152]{2,1,0:T(8,128)(2,1)S(1)}, bf16[2,184,1152]{2,1,0:T(8,128)(2,1)}, u32[]{:S(2)}) copy-start(bf16[2,184,1152]{2,1,0:T(8,128)(2,1)} %param.33) | copy-start | bytes 2543620
  11.9 207.3 %all-gather.14.cloned.1.call-start = ((), (), s32[]{:S(2)}) async-start(), calls=%async_computation.10 | async-start | bytes 6266880 | tf_op jit(solution)/shard_map/all_gather | solution.py:43
  64.0 155.2 %collective-permute-start = (bf16[4,144,3456]{2,1,0:T(8,128)(2,1)}, bf16[4,144,3456]{2,1,0:T(8,128)(2,1)}, u32[]{:S(2)}, u32[]{:S(2)}) collective-permute-start(bf16[4,144,3456]{2,1,0:T(8,128)(2,1)} %bitcast.221), channel_id=1, source_target_pairs={{0,4},{4,0},{1,5},{5,1},{2,6},{6,2},{3,7},{7,3},{8,12},{12,8},{9,1... | collective-permute-start | bytes 11943944 | tf_op jit(solution)/shard_map/ppermute | solution.py:31
  84.7 139.5 %copy-start.36 = (f32[2,184]{1,0:T(2,128)}, f32[2,184]{1,0:T(2,128)S(1)}, u32[]{:S(2)}) copy-start(f32[2,184]{1,0:T(2,128)S(1)} %broadcast_multiply_fusion.1) | copy-start | bytes 4420
  95.6 149.8 %collective-permute-start.1 = (bf16[4,144,1152]{2,1,0:T(8,128)(2,1)}, bf16[4,144,1152]{2,1,0:T(8,128)(2,1)}, u32[]{:S(2)}, u32[]{:S(2)}) collective-permute-start(bf16[4,144,1152]{2,1,0:T(8,128)(2,1)} %bitcast.234), channel_id=1, source_target_pairs={{0,4},{4,0},{1,5},{5,1},{2,6},{6,2},{3,7},{7,3},{8,12},{12,8},{9,1... | collective-permute-start | bytes 3981320 | tf_op jit(solution)/shard_map/ppermute | solution.py:31
  157.5 91.7 %collective-permute-start.3 = (bf16[4,144,4304]{2,1,0:T(8,128)(2,1)}, bf16[4,144,4304]{2,1,0:T(8,128)(2,1)}, u32[]{:S(2)}, u32[]{:S(2)}) collective-permute-start(bf16[4,144,4304]{2,1,0:T(8,128)(2,1)} %bitcast.215), channel_id=1, source_target_pairs={{0,4},{4,0},{1,5},{5,1},{2,6},{6,2},{3,7},{7,3},{8,12},{12,8},{9,1... | collective-permute-start | bytes 14874632 | tf_op jit(solution)/shard_map/ppermute | solution.py:31
  219.2 38.5 %collective-permute-start.2 = (bf16[4,144,4304]{2,1,0:T(8,128)(2,1)}, bf16[4,144,4304]{2,1,0:T(8,128)(2,1)}, u32[]{:S(2)}, u32[]{:S(2)}) collective-permute-start(bf16[4,144,4304]{2,1,0:T(8,128)(2,1)} %bitcast.217), channel_id=1, source_target_pairs={{0,4},{4,0},{1,5},{5,1},{2,6},{6,2},{3,7},{7,3},{8,12},{12,8},{9,1... | collective-permute-start | bytes 14874632 | tf_op jit(solution)/shard_map/ppermute | solution.py:31
  240.5 44.4 %all-to-all-start = ((bf16[4,3,2,184,288]{4,3,2,1,0:T(8,128)(2,1)}), bf16[4,3,2,184,288]{4,3,2,1,0:T(8,128)(2,1)}, u32[]{:S(2)}, u32[]{:S(2)}) async-start(bf16[4,3,2,184,288]{4,3,2,1,0:T(8,128)(2,1)} %pad_maximum_fusion.5), calls=%async_computation | async-start | bytes 6782976 | tf_op jit(solution)/shard_map/all_to_all | solution.py:126
  328.2 30.1 %all-to-all-start.1 = ((bf16[2,736,288]{2,0,1:T(2,128)(2,1)}), bf16[2,736,288]{2,0,1:T(2,128)(2,1)}, u32[]{:S(2)}, u32[]{:S(2)}) async-start(bf16[2,736,288]{2,0,1:T(2,128)(2,1)} %copy.99), calls=%async_computation.1 | async-start | bytes 2260992 | tf_op jit(solution)/shard_map/all_to_all | solution.py:139
  367.3 39.8 %copy-start.5 = (f32[368,1152]{1,0:T(8,128)}, f32[368,1152]{1,0:T(8,128)S(1)}, u32[]{:S(2)}) copy-start(f32[368,1152]{1,0:T(8,128)S(1)} %get-tuple-element.89) | copy-start | bytes 5087236
  367.4 8.8 slice-start
  367.7 8.5 slice-start.1
  367.7 8.5 slice-start.2
  367.7 8.5 copy-start.29
  376.1 11.0 %copy-start.13 = (f32[368,4304]{1,0:T(8,128)}, f32[368,4304]{1,0:T(8,128)S(1)}, u32[]{:S(2)}) copy-start(f32[368,4304]{1,0:T(8,128)S(1)} %convolution_add_fusion) | copy-start | bytes 19006468
  387.1 10.1 %copy-start.25 = (bf16[368,4304]{1,0:T(8,128)(2,1)S(1)}, bf16[368,4304]{1,0:T(8,128)(2,1)}, u32[]{:S(2)}) copy-start(bf16[368,4304]{1,0:T(8,128)(2,1)} %get-tuple-element.36) | copy-start | bytes 9503236
  416.5 20.4 %all-to-all-start.2 = ((bf16[2,184,1152]{1,0,2:T(2,128)(2,1)}), bf16[2,184,1152]{1,0,2:T(2,128)(2,1)}, u32[]{:S(2)}, u32[]{:S(2)}) async-start(bf16[2,184,1152]{1,0,2:T(2,128)(2,1)} %copy.105), calls=%async_computation.2 | async-start | bytes 2359296 | tf_op jit(solution)/shard_map/all_to_all | solution.py:171
  429.7 80.3 %collective-permute-start.6 = (bf16[4,144,1152]{2,1,0:T(8,128)(2,1)}, bf16[4,144,1152]{2,1,0:T(8,128)(2,1)}, u32[]{:S(2)}, u32[]{:S(2)}) collective-permute-start(bf16[4,144,1152]{2,1,0:T(8,128)(2,1)} %fusion.40), channel_id=1, source_target_pairs={{0,4},{4,0},{1,5},{5,1},{2,6},{6,2},{3,7},{7,3},{8,12},{12,8},{9,1... | collective-permute-start | bytes 3981320 | tf_op jit(solution)/shard_map/ppermute | solution.py:31
  436.8 76.8 %collective-permute-start.8 = (bf16[4,144,4304]{2,1,0:T(8,128)(2,1)}, bf16[4,144,4304]{2,1,0:T(8,128)(2,1)}, u32[]{:S(2)}, u32[]{:S(2)}) collective-permute-start(bf16[4,144,4304]{2,1,0:T(8,128)(2,1)} %fusion.13), channel_id=1, source_target_pairs={{0,4},{4,0},{1,5},{5,1},{2,6},{6,2},{3,7},{7,3},{8,12},{12,8},{9,1... | collective-permute-start | bytes 14874632 | tf_op jit(solution)/shard_map/ppermute | solution.py:31
  455.6 12.3 %copy-start.28 = (bf16[2,736,4,72]{1,3,2,0:T(8,128)(2,1)S(1)}, bf16[2,736,4,72]{1,3,2,0:T(8,128)(2,1)}, u32[]{:S(2)}) copy-start(bf16[2,736,4,72]{1,3,2,0:T(8,128)(2,1)} %reshape.306) | copy-start | bytes 2543620
  467.9 9.9 %copy-start.21 = (bf16[2,736,4,72]{1,3,2,0:T(8,128)(2,1)S(1)}, bf16[2,736,4,72]{1,3,2,0:T(8,128)(2,1)}, u32[]{:S(2)}) copy-start(bf16[2,736,4,72]{1,3,2,0:T(8,128)(2,1)} %squeeze.70) | copy-start | bytes 2543620
  484.2 9.6 copy-start.14
  505.3 44.3 %all-to-all-start.3 = ((bf16[3,2,736,288]{3,1,0,2:T(2,128)(2,1)}), bf16[3,2,736,288]{3,1,0,2:T(2,128)(2,1)}, u32[]{:S(2)}, u32[]{:S(2)}) async-start(bf16[3,2,736,288]{3,1,0,2:T(2,128)(2,1)} %pad_maximum_fusion.6), calls=%async_computation.3 | async-start | bytes 6782976 | tf_op jit(solution)/shard_map/all_to_all | solution.py:187
  510.0 154.3 %reduce-scatter.15.cloned.1.call-start = ((), (), s32[]{:S(2)}) async-start(), calls=%async_computation.13 | async-start | bytes 1658880
  513.5 150.8 %reduce-scatter.17.cloned.1.call-start = ((), (), s32[]{:S(2)}) async-start(), calls=%async_computation.14 | async-start | bytes 6266880
  522.3 157.0 %reduce-scatter.13.cloned.1.call-start = ((), (), s32[]{:S(2)}) async-start(), calls=%async_computation.12 | async-start | bytes 4976640
  587.7 7.6 copy-start.19
  587.7 7.6 copy-start.10
  587.7 7.6 copy-start.32
  587.7 7.6 copy-start.34
  613.2 8.7 collective-permute-start.4
  629.0 113.4 %reduce-scatter.19.cloned.1.call-start = ((), (), s32[]{:S(2)}) async-start(), calls=%async_computation.15 | async-start | bytes 6266880
  646.1 9.1 collective-permute-start.10
  664.0 78.4 %copy-start.39 = (f32[4,288]{1,0:T(4,128)S(1)}, f32[4,288]{1,0:T(4,128)}, u32[]{:S(2)}) copy-start(f32[4,288]{1,0:T(4,128)} %get-tuple-element.75) | copy-start | bytes 13828
  664.0 78.5 %copy-start.35 = (f32[1152]{0:T(1024)S(1)}, f32[1152]{0:T(1024)}, u32[]{:S(2)}) copy-start(f32[1152]{0:T(1024)} %get-tuple-element.72) | copy-start | bytes 13828
  664.1 224.4 %all-reduce.9.cloned.1.call-start = ((), (), s32[]{:S(2)}) async-start(), calls=%async_computation.16 | async-start | bytes 7667712 | tf_op jit(solution)/shard_map/psum | solution.py:58
  742.4 148.8 %copy-start.6 = (f32[368,1152]{1,0:T(8,128)S(1)}, f32[368,1152]{1,0:T(8,128)}, u32[]{:S(2)}) copy-start(f32[368,1152]{1,0:T(8,128)} %copy-done.5) | copy-start | bytes 5087236
  891.1 11.3 %copy-start.38 = (f32[1152]{0:T(1024)S(1)}, f32[1152]{0:T(1024)}, u32[]{:S(2)}) copy-start(f32[1152]{0:T(1024)} %get-tuple-element.37) | copy-start | bytes 13828
  891.1 11.3 %copy-start.43 = (f32[1152]{0:T(1024)S(1)}, f32[1152]{0:T(1024)}, u32[]{:S(2)}) copy-start(f32[1152]{0:T(1024)} %get-tuple-element.17) | copy-start | bytes 13828
  891.1 11.4 %copy-start.42 = (f32[1152]{0:T(1024)S(1)}, f32[1152]{0:T(1024)}, u32[]{:S(2)}) copy-start(f32[1152]{0:T(1024)} %get-tuple-element.19) | copy-start | bytes 13828
  891.1 11.5 %copy-start.40 = (f32[4304]{0:T(1024)S(1)}, f32[4304]{0:T(1024)}, u32[]{:S(2)}) copy-start(f32[4304]{0:T(1024)} %get-tuple-element.35) | copy-start | bytes 51652
  891.1 65.9 %collective-permute-start.5 = (f32[1,144,3456]{2,1,0:T(8,128)}, f32[1,144,3456]{2,1,0:T(8,128)}, u32[]{:S(2)}, u32[]{:S(2)}) collective-permute-start(f32[1,144,3456]{2,1,0:T(8,128)} %convert_element_type.225), channel_id=1, source_target_pairs={{0,4},{4,0},{1,5},{5,1},{2,6},{6,2},{3,7},{7,3},{8,12},{12,8},{9,1... | collective-permute-start | bytes 5971976 | tf_op jit(solution)/shard_map/ppermute | solution.py:31
  902.3 21.5 %copy-start.27 = (bf16[1,144,1152]{2,1,0:T(8,128)(2,1)S(1)}, bf16[1,144,1152]{2,1,0:T(8,128)(2,1)}, u32[]{:S(2)}) copy-start(bf16[1,144,1152]{2,1,0:T(8,128)(2,1)} %get-tuple-element.32) | copy-start | bytes 995332
  902.3 52.4 %copy-start.17 = (bf16[1,144,4304]{2,1,0:T(8,128)(2,1)S(1)}, bf16[1,144,4304]{2,1,0:T(8,128)(2,1)}, u32[]{:S(2)}) copy-start(bf16[1,144,4304]{2,1,0:T(8,128)(2,1)} %get-tuple-element.33) | copy-start | bytes 3718660
  905.8 49.2 %copy-start.15 = (bf16[1,144,4304]{2,1,0:T(8,128)(2,1)S(1)}, bf16[1,144,4304]{2,1,0:T(8,128)(2,1)}, u32[]{:S(2)}) copy-start(bf16[1,144,4304]{2,1,0:T(8,128)(2,1)} %get-tuple-element.34) | copy-start | bytes 3718660
  924.7 31.0 %collective-permute-start.7 = (f32[1,144,1152]{2,1,0:T(8,128)}, f32[1,144,1152]{2,1,0:T(8,128)S(1)}, u32[]{:S(2)}, u32[]{:S(2)}) collective-permute-start(f32[1,144,1152]{2,1,0:T(8,128)} %convert_element_type.230), channel_id=1, source_target_pairs={{0,4},{4,0},{1,5},{5,1},{2,6},{6,2},{3,7},{7,3},{8,12},{12,8},{9,1... | collective-permute-start | bytes 1990664 | tf_op jit(solution)/shard_map/ppermute | solution.py:31
  954.9 6.1 collective-permute-start.9
  955.1 8.8 collective-permute-start.11
  (20 other events, 51.0 us)
Sparse Core Ops, SparseCore 0:
  10.4 53.5 all-gather.9
  66.4 29.1 all-gather.11
  98.1 59.3 all-gather.15
  159.7 59.3 all-gather.13
  514.1 30.3 reduce-scatter.14
  548.0 59.3 reduce-scatter.16
  629.1 50.1 reduce-scatter.12
  682.9 59.4 reduce-scatter.18
  745.0 143.3 all-reduce.8
